TPU v7x, 32 devices: a whole 2x2x4 slice. The times are simulated.
32 devices in a mesh: dp: 8 (over y, x, core), tensor: 4 (over z).
Axes of the slice: x: 2, y: 2, z: 4, core: 2. Of those that a mesh axis runs over, the one named last changes fastest.
Arguments:
- attn_out: bfloat16 [8192, 3072], P('dp', 'tensor'), may hold values from -6 to 6
- cotangent: bfloat16 [8192, 2560], P(('dp', 'tensor')), may hold values from -0.1875 to 0.1875
- residual: bfloat16 [8, 3072, 2560], P('dp', 'tensor'), may hold values from -6 to 6
- local_offsets: int32 [8, 4, 8, 48], P('dp', 'tensor'), may hold values from 0 to 2399, as said below
- local_counts: int32 [8, 4, 8], P('dp', 'tensor'), may hold values from 1 to 48, as said below
- kept_offsets: int32 [4, 8, 12], P('tensor'), may hold values from 0 to 2399, as said below
- kept_counts: int32 [4, 8], P('tensor'), may hold values from 6 to 12, as said below
- bounds: int32 [9], replicated, may hold values from 0 to 15360, as said below
Outputs:
- new_residual: bfloat16 [8, 3072, 2560], P('dp', 'tensor')
- kept_sums: float32 [4, 8, 12, 128], P('tensor')
Inputs may be any that keep to these rules, and one draw needn't show every extreme that they name: `local_offsets`: for each replica, band and region the 48 entries are different offsets within the region (below bounds[r + 1] - bounds[r]); slots at or past local_counts are ignored but hold such offsets too. `local_counts`: for each band, some region has 48 live slots from every replica. `kept_offsets`: for each band and region the 12 entries are different offsets within the region; slots at or past kept_counts are ignored. `kept_counts`: for each band, some region has 12 live kept slots. bounds[0] = 0, bounds[8] = 15360, rising; each region holds 1440 to 2400 blocks.
All inputs are finite; a program needn't handle non-finite values.
Results may differ from a plain program's by a relative error of at most 0.001.
Values may be sent and summed in bfloat16 or wider, within the bound.
No kernel may reach another device: no remote copies, remote signals or barrier semaphores. Data moves between devices by JAX's collectives and lax.ppermute only.
A program may use at most 64 MiB of HBM per device.

v0:
```python
import jax
import jax.numpy as jnp
from jax import lax
from jax.sharding import PartitionSpec as P


def on_device(
    attn_out, cotangent, residual, local_offsets, local_counts, kept_offsets, kept_counts, bounds
):
    gradient = lax.dot_general(
        attn_out,
        lax.all_gather(cotangent, "tensor", axis=0, tiled=True),
        (((0,), (0,)), ((), ())),
        preferred_element_type=jnp.float32,
    )
    accumulated = residual[0].astype(jnp.float32) + gradient
    blocks = accumulated.reshape(-1, 128)
    regions = local_offsets.shape[2]
    slot_count = local_offsets.shape[3]
    offsets = local_offsets[0, 0]
    counts = local_counts[0, 0]
    live_slots = jnp.arange(slot_count)[None, :] < counts[:, None]
    region_starts = bounds[:regions]
    where_abs = region_starts[:, None] + offsets
    picked = blocks[where_abs] * live_slots[..., None].astype(jnp.float32)
    sent_mask = (
        jnp.zeros((blocks.shape[0],), jnp.float32)
        .at[where_abs.reshape(-1)]
        .max(live_slots.reshape(-1).astype(jnp.float32))
    )
    new_residual = (
        (blocks * (1.0 - sent_mask[:, None])).reshape(accumulated.shape).astype(jnp.bfloat16)[None]
    )
    kept_here = kept_offsets[0]
    kept_live = jnp.arange(kept_here.shape[1])[None, :] < kept_counts[0][:, None]
    moved, moved_offsets = (
        lax.all_to_all(picked, "dp", split_axis=0, concat_axis=0, tiled=True),
        lax.all_to_all(offsets.astype(jnp.float32), "dp", split_axis=0, concat_axis=0, tiled=True),
    )
    owner_index = lax.axis_index("dp")
    own_kept = lax.dynamic_index_in_dim(kept_here, owner_index, 0, keepdims=False)
    own_live = lax.dynamic_index_in_dim(kept_live, owner_index, 0, keepdims=False)
    matches = (
        (own_kept[:, None].astype(jnp.float32) == moved_offsets.reshape(1, -1)) & own_live[:, None]
    ).astype(jnp.float32)
    owned = jnp.dot(
        matches,
        moved.reshape(-1, 128),
        precision=lax.Precision.HIGHEST,
        preferred_element_type=jnp.float32,
    )[None]
    summed = lax.all_gather(owned, "dp", axis=0, tiled=True)
    return (new_residual, summed[None])


def solution(mesh):
    in_specs = (
        P("dp", "tensor"),
        P(("dp", "tensor"), None),
        P("dp", "tensor", None),
        P("dp", "tensor", None, None),
        P("dp", "tensor", None),
        P("tensor", None, None),
        P("tensor", None),
        P(),
    )
    out_specs = (P("dp", "tensor", None), P("tensor", None, None, None))
    return jax.shard_map(
        on_device, mesh=mesh, in_specs=in_specs, out_specs=out_specs, check_vma=False
    )
```

profile of v0, /device:TPU:0, one launch (start us, length us, event | category | flops | bytes accessed | tf_op | source)
XLA Modules:
  0.0 163.7 jit_solution(15876874324029748088)
XLA Ops:
  7.2 0.0 copy-start
  7.2 0.0 all-gather.4.cloned.1.call-start
  7.2 0.7 all-gather.4.cloned.1.call-update
  7.9 1.3 convert_element_type.55
  9.2 5.2 %all-to-all-start = ((f32[8,1,48]{2,1,0:T(1,128)}), f32[8,1,48]{2,1,0:T(1,128)S(1)}, u32[]{:S(2)}, u32[]{:S(2)}) async-start(f32[8,1,48]{2,1,0:T(1,128)} %bitcast.5), calls=%async_computation | async-start | bytes 8192 | tf_op jit(solution)/shard_map/all_to_all | solution.py:38
  14.4 0.8 squeeze.11
  15.2 0.7 add.65
  15.9 0.1 add.66
  16.0 0.7 fusion.8
  16.7 0.1 reshape.165
  16.8 0.8 compare_select_fusion
  17.5 0.1 reshape.155
  17.7 3.3 %scatter_custom_fusion = f32[15360]{0:T(1024)S(1)} fusion(s32[384]{0:T(512)S(1)} %fusion.9, f32[384]{0:T(512)S(1)} %reshape.165, f32[]{:T(128)} %constant.8.clone.1), kind=kCustom, calls=%fused_computation.7 | custom fusion | flops 384 | bytes 61444 | tf_op jit(solution)/shard_map/scatter-max | solution.py:29
  21.0 0.7 convert_bitcast_fusion
  21.7 0.7 iota_compare_fusion
  22.4 0.4 mul.21
  22.9 0.2 copy.14
  23.0 3.8 %mul.22 = f32[768,20,128]{0,2,1:T(8,128)} broadcast(f32[768,20]{0,1:T(8,128)S(1)} %copy.14), dimensions={0,1} | broadcast | bytes 7925760 | tf_op jit(solution)/shard_map/mul | solution.py:32
  26.8 9.2 %copy.15 = f32[768,2560]{1,0:T(8,128)} copy(f32[768,2560]{0,1:T(8,128)} %bitcast.30) | data formatting | bytes 15728640 | tf_op jit(solution)/shard_map/mul | solution.py:32
  36.0 0.0 all-to-all-done
  36.0 0.5 broadcast.78
  36.5 0.7 reduce.5
  37.1 0.1 eq.16
  37.2 73.2 %all-gather.4.cloned.1.call-done = bf16[1024,2560]{1,0:T(8,128)(2,1)} async-done(((bf16[256,2560]{1,0:T(8,128)(2,1)}), bf16[1024,2560]{1,0:T(8,128)(2,1)}) %all-gather.4.cloned.1.call-update) | async-done | bytes 5242896 | tf_op jit(solution)/shard_map/all_gather | solution.py:12
  110.4 0.0 copy-done
  110.4 9.6 %convert_add_fusion = f32[768,2560]{1,0:T(8,128)} fusion(bf16[1024,768]{1,0:T(8,128)(2,1)S(1)} %copy-done, bf16[1024,2560]{1,0:T(8,128)(2,1)} %all-gather.4.cloned.1.call-done, bf16[1,768,2560]{2,1,0:T(8,128)(2,1)} %param.10), kind=kOutput, calls=%fused_computation.2 | convolution fusion | flops 4030464000 | bytes 18612224 | tf_op jit(solution)/shard_map/dot_general | solution.py:10
  120.0 8.9 %reshape.149 = f32[15360,128]{1,0:T(8,128)} reshape(f32[768,2560]{1,0:T(8,128)} %convert_add_fusion) | data formatting | bytes 15728640 | tf_op jit(solution)/shard_map/reshape | solution.py:17
  128.9 4.3 %gather_fusion = f32[384,128]{1,0:T(8,128)S(1)} fusion(f32[15360,128]{1,0:T(8,128)} %reshape.149, s32[1024]{0:T(1024)S(1)} %pad_clamp_fusion), kind=kCustom, calls=%fused_computation | custom fusion | bytes 394752 | tf_op jit(solution)/shard_map/gather | solution.py:25
  133.2 0.8 broadcast_multiply_fusion
  134.0 3.6 %all-to-all-start.1 = ((f32[8,48,128]{2,1,0:T(8,128)}), f32[8,48,128]{2,1,0:T(8,128)S(1)}, u32[]{:S(2)}, u32[]{:S(2)}) async-start(f32[8,48,128]{2,1,0:T(8,128)} %broadcast_multiply_fusion), calls=%async_computation.1 | async-start | bytes 393216 | tf_op jit(solution)/shard_map/all_to_all | solution.py:37
  137.6 8.6 %fusion = bf16[1,768,2560]{2,1,0:T(8,128)(2,1)} fusion(f32[768,2560]{1,0:T(8,128)} %convert_add_fusion, f32[768,2560]{1,0:T(8,128)} %copy.15), kind=kLoop, calls=%fused_computation.4 | loop fusion | flops 3932160 | bytes 19660800 | tf_op jit(solution)/shard_map/broadcast_in_dim | solution.py:32
  146.2 0.0 all-to-all-done.1
  146.2 0.2 convolution_bitcast_fusion
  146.4 9.8 %all-gather.1 = f32[8,12,128]{2,1,0:T(8,128)S(1)} all-gather(f32[1,12,128]{2,1,0:T(8,128)S(1)} %convolution_bitcast_fusion), channel_id=2, replica_groups=mesh['dp'=8,'tensor'=4] {'dp'}, dimensions={0}, use_global_device_ids=true | all-gather | bytes 55296 | tf_op jit(solution)/shard_map/all_gather | solution.py:52
  156.2 0.6 copy.16
  (4 shorter events, 0.0 us)
Async XLA Ops:
  7.2 103.2 %copy-start = (bf16[1024,768]{1,0:T(8,128)(2,1)S(1)}, bf16[1024,768]{1,0:T(8,128)(2,1)}, u32[]{:S(2)}) copy-start(bf16[1024,768]{1,0:T(8,128)(2,1)} %param.8) | copy-start | bytes 4718596
  7.2 103.2 %all-gather.4.cloned.1.call-start = ((), (), s32[]{:S(2)}) async-start(), calls=%async_computation.2 | async-start | bytes 6553600 | tf_op jit(solution)/shard_map/all_gather | solution.py:12
  9.2 26.8 %all-to-all-start = ((f32[8,1,48]{2,1,0:T(1,128)}), f32[8,1,48]{2,1,0:T(1,128)S(1)}, u32[]{:S(2)}, u32[]{:S(2)}) async-start(f32[8,1,48]{2,1,0:T(1,128)} %bitcast.5), calls=%async_computation | async-start | bytes 8192 | tf_op jit(solution)/shard_map/all_to_all | solution.py:38
  134.0 12.2 %all-to-all-start.1 = ((f32[8,48,128]{2,1,0:T(8,128)}), f32[8,48,128]{2,1,0:T(8,128)S(1)}, u32[]{:S(2)}, u32[]{:S(2)}) async-start(f32[8,48,128]{2,1,0:T(8,128)} %broadcast_multiply_fusion), calls=%async_computation.1 | async-start | bytes 393216 | tf_op jit(solution)/shard_map/all_to_all | solution.py:37
Sparse Core Ops, SparseCore 0:
  9.6 100.7 all-gather.3
where the time goes:
time: 164 us
  waiting for transfers between devices  73.8 us (45%)
  local copies, waits for them, and re-layouts  29.8 us (18%)
  other arithmetic  17.6 us (11%)
  between operations  14.1 us (9%)
  matrix products  9.78 us (6%)
  blocking collectives  9.76 us (6%)
  starting transfers between devices  8.85 us (5%)
    all_gather x1, waiting for transfers between devices, on_device(): lax.all_gather(cotangent, 'tensor', axis=0, tiled=True)  73.2 us
    mul x4, local copies, waits for them, and re-layouts, on_device(): blocks * (1.0 - sent_mask[:, None])  13.5 us
    all_gather x1, blocking collectives, on_device(): summed = lax.all_gather(owned, 'dp', axis=0, tiled=True)  9.76 us
    dot_general x1, matrix products, on_device(): lax.dot_general(attn_out, lax.all_gather(cotangent, 'tensor', axis=0, til...  9.57 us
    reshape x1, local copies, waits for them, and re-layouts, on_device(): blocks = accumulated.reshape(-1, 128)  8.91 us
    broadcast_in_dim x1, other arithmetic, on_device(): (blocks * (1.0 - sent_mask[:, None])).reshape(accumulated.shape)  8.58 us
    all_to_all x1, starting transfers between devices, on_device(): lax.all_to_all(offsets.astype(jnp.float32), 'dp', split_axis=0, concat_ax...  5.2 us
    gather x1, local copies, waits for them, and re-layouts, on_device(): picked = blocks[where_abs] * live_slots[..., None].astype(jnp.float32)  4.35 us
  transfers between devices with their start and end apart: 3, of which 1 were waited for; matrix products, arithmetic and copies ran while one was open for 20% of the time, Pallas kernels for 0%

commit v1 on v0

v1 whole, which is shorter than its diff:
```python
import functools

import jax
import jax.numpy as jnp
from jax import lax
from jax.experimental import pallas as pl
from jax.experimental.pallas import tpu as pltpu
from jax.sharding import PartitionSpec as P

LANES = 128


def dot(a, b):
    return lax.dot_general(a, b, (((1,), (0,)), ((), ())), preferred_element_type=jnp.float32)


def first_kernel(index_ref, attn_ref, piece_ref, residual_ref, out_ref):
    out_ref[...] = residual_ref[...].astype(jnp.float32) + dot(attn_ref[...], piece_ref[...])


def add_kernel(index_ref, attn_up_ref, attn_down_ref, up_ref, down_ref, acc_ref, out_ref):
    out_ref[...] = acc_ref[...] + (
        dot(attn_up_ref[...], up_ref[...]) + dot(attn_down_ref[...], down_ref[...])
    )


def last_kernel(index_ref, attn_ref, up_ref, down_ref, acc_ref, sent_ref, *rest, first):
    out_ref = rest[-1]
    total = acc_ref[...] + dot(attn_ref[...], up_ref[...] + down_ref[...])
    width = total.shape[1]
    block = pl.program_id(0) * (width // LANES) + first
    spread = (
        lax.broadcasted_iota(jnp.int32, (LANES, width), 0)
        == lax.broadcasted_iota(jnp.int32, (LANES, width), 1) // LANES + block
    ).astype(jnp.bfloat16)
    sent = dot(sent_ref[...], spread)
    out_ref[...] = jnp.where(sent > 0.5, 0.0, total).astype(out_ref.dtype)


def tile_of(width):
    for tile in (512, 384, 256, 128):
        if width % tile == 0:
            return tile
    return width


def first_step(where, attn_t, piece, residual, column):
    rows, tokens = attn_t.shape[0], piece.shape[0]
    width = piece.shape[1]
    tile = tile_of(width)
    base = column // tile
    return pl.pallas_call(
        first_kernel,
        grid_spec=pltpu.PrefetchScalarGridSpec(
            num_scalar_prefetch=1,
            grid=(width // tile,),
            in_specs=[
                pl.BlockSpec((rows, tokens), lambda i, w: (0, w[0])),
                pl.BlockSpec((tokens, tile), lambda i, w: (0, i)),
                pl.BlockSpec((rows, tile), lambda i, w: (0, i + base)),
            ],
            out_specs=pl.BlockSpec((rows, tile), lambda i, w: (0, i)),
        ),
        out_shape=jax.ShapeDtypeStruct((rows, width), jnp.float32),
        cost_estimate=pl.CostEstimate(
            flops=2 * rows * width * tokens, bytes_accessed=6 * rows * width, transcendentals=0
        ),
    )(where, attn_t, piece, residual)


def add_step(where, attn_t, up, down, acc):
    rows, tokens = attn_t.shape[0], up.shape[0]
    width = up.shape[1]
    tile = tile_of(width)
    return pl.pallas_call(
        add_kernel,
        grid_spec=pltpu.PrefetchScalarGridSpec(
            num_scalar_prefetch=1,
            grid=(width // tile,),
            in_specs=[
                pl.BlockSpec((rows, tokens), lambda i, w: (0, w[0])),
                pl.BlockSpec((rows, tokens), lambda i, w: (0, w[1])),
                pl.BlockSpec((tokens, tile), lambda i, w: (0, i)),
                pl.BlockSpec((tokens, tile), lambda i, w: (0, i)),
                pl.BlockSpec((rows, tile), lambda i, w: (0, i)),
            ],
            out_specs=pl.BlockSpec((rows, tile), lambda i, w: (0, i)),
        ),
        out_shape=jax.ShapeDtypeStruct((rows, width), jnp.float32),
        input_output_aliases={5: 0},
        cost_estimate=pl.CostEstimate(
            flops=4 * rows * width * tokens, bytes_accessed=8 * rows * width, transcendentals=0
        ),
    )(where, attn_t, attn_t, up, down, acc)


def last_step(where, attn_t, up, down, acc, sent, column, columns, before):
    rows, tokens = attn_t.shape[0], up.shape[0]
    width = up.shape[1]
    tile = tile_of(width)
    base = column // tile
    in_specs = [
        pl.BlockSpec((rows, tokens), lambda i, w: (0, w[0])),
        pl.BlockSpec((tokens, tile), lambda i, w: (0, i)),
        pl.BlockSpec((tokens, tile), lambda i, w: (0, i)),
        pl.BlockSpec((rows, tile), lambda i, w: (0, i)),
        pl.BlockSpec((rows, LANES), lambda i, w: (0, 0)),
    ]
    operands = [where, attn_t, up, down, acc, sent]
    aliases = {}
    if before is not None:
        in_specs.append(pl.BlockSpec(memory_space=pl.ANY))
        operands.append(before)
        aliases = {len(operands) - 1: 0}
    return pl.pallas_call(
        functools.partial(last_kernel, first=column // LANES),
        grid_spec=pltpu.PrefetchScalarGridSpec(
            num_scalar_prefetch=1,
            grid=(width // tile,),
            in_specs=in_specs,
            out_specs=pl.BlockSpec((rows, tile), lambda i, w: (0, i + base)),
        ),
        out_shape=jax.ShapeDtypeStruct((rows, columns), jnp.bfloat16),
        input_output_aliases=aliases,
        cost_estimate=pl.CostEstimate(
            flops=2 * rows * width * tokens, bytes_accessed=6 * rows * width, transcendentals=0
        ),
    )(*operands)


def on_device(
    ranks,
    attn_out,
    cotangent,
    residual,
    local_offsets,
    local_counts,
    kept_offsets,
    kept_counts,
    bounds,
):
    me = lax.axis_index("tensor")
    tokens, columns = cotangent.shape
    rows = attn_out.shape[1]
    col_blocks = columns // LANES
    cut = (columns // LANES // 2) * LANES
    chunks = [(0, cut), (cut, columns)]

    own = [cotangent[:, a:b] for a, b in chunks]
    ups, downs = [own], [own]
    for step in range(1, ranks):
        ups.append(
            [lax.ppermute(x, "tensor", [(i, i + 1) for i in range(step - 1, ranks - 1)]) for x in ups[-1]]
        )
        downs.append(
            [lax.ppermute(x, "tensor", [(i, i - 1) for i in range(1, ranks - step + 1)]) for x in downs[-1]]
        )

    attn_t = attn_out.T
    res = residual[0]
    regions, slots = local_offsets.shape[2:]
    starts = bounds[:regions]
    offsets, counts = local_offsets[0, 0], local_counts[0, 0]
    live = jnp.arange(slots)[None, :] < counts[:, None]
    where_abs = (starts[:, None] + offsets).reshape(-1)
    row_hot = (
        (where_abs // col_blocks)[:, None] == jnp.arange(rows)[None, :]
    ) & live.reshape(-1)[:, None]
    col_hot = (where_abs % col_blocks)[:, None] == jnp.arange(LANES)[None, :]
    sent = lax.dot_general(
        row_hot.astype(jnp.bfloat16),
        col_hot.astype(jnp.bfloat16),
        (((0,), (0,)), ((), ())),
        preferred_element_type=jnp.float32,
    ).astype(jnp.bfloat16)

    kept, kept_total = kept_offsets[0], kept_counts[0]
    caps = kept.shape[1]
    kept_live = jnp.arange(caps)[None, :] < kept_total[:, None]
    found = jnp.any((kept[:, :, None] == offsets[:, None, :]) & live[:, None, :], axis=2) & kept_live
    kept_abs = (starts[:, None] + kept).reshape(-1)
    kept_row_hot = (
        ((kept_abs // col_blocks)[:, None] == jnp.arange(rows)[None, :]) & found.reshape(-1)[:, None]
    ).astype(jnp.bfloat16)
    kept_col_hot = ((kept_abs % col_blocks)[:, None] == jnp.arange(col_blocks)[None, :]).astype(jnp.float32)
    lists = kept_abs.shape[0]
    kept_attn = lax.dot_general(
        kept_row_hot, attn_out, (((1,), (1,)), ((), ())), preferred_element_type=jnp.float32
    ).astype(jnp.bfloat16)

    def rank_slice(rank):
        return lax.dynamic_slice_in_dim(kept_attn, lax.rem(rank + ranks, ranks) * tokens, tokens, 1)

    picked = []
    accs = []
    for h, (a, b) in enumerate(chunks):
        acc = first_step(me[None], attn_t, own[h], res, a)
        wide = dot(kept_row_hot, res[:, a:b]) + dot(rank_slice(me), own[h])
        for step in range(1, ranks):
            wide = wide + dot(rank_slice(me - step), ups[step][h]) + dot(rank_slice(me + step), downs[step][h])
            if step < ranks - 1:
                where = jnp.stack([lax.rem(me - step + ranks, ranks), lax.rem(me + step, ranks)])
                acc = add_step(where, attn_t, ups[step][h], downs[step][h], acc)
        accs.append(acc)
        hot = kept_col_hot[:, a // LANES : b // LANES]
        picked.append(jnp.sum(wide.reshape(lists, -1, LANES) * hot[:, :, None], axis=1))
    far = jnp.where(me == 0, ranks - 1, 0)[None]
    out = None
    for h, (a, b) in enumerate(chunks):
        out = last_step(far, attn_t, ups[-1][h], downs[-1][h], accs[h], sent, a, columns, out)

    mine = functools.reduce(jnp.add, picked)
    every = lax.all_gather(mine, "dp", axis=0)
    summed = jnp.sum(every, axis=0)
    return (out[None], summed.reshape(1, regions, caps, LANES))


def solution(mesh):
    in_specs = (
        P("dp", "tensor"),
        P(("dp", "tensor"), None),
        P("dp", "tensor", None),
        P("dp", "tensor", None, None),
        P("dp", "tensor", None),
        P("tensor", None, None),
        P("tensor", None),
        P(),
    )
    out_specs = (P("dp", "tensor", None), P("tensor", None, None, None))
    return jax.shard_map(
        functools.partial(on_device, mesh.shape["tensor"]),
        mesh=mesh,
        in_specs=in_specs,
        out_specs=out_specs,
        check_vma=False,
    )
```

time: 164 us -> 136 us (0.83)
  waiting for transfers between devices: 73.8 us -> 10.5 us
  Pallas kernels: 0 us -> 56.5 us
  local copies, waits for them, and re-layouts: 29.8 us -> 8.31 us
  other arithmetic: 17.6 us -> 1.91 us
  matrix products: 9.78 us -> 24.9 us
  between operations: 14.1 us -> 1.14 us
  starting transfers between devices: 8.85 us -> 21.6 us
    all_gather x1 -> x0, waiting for transfers between devices: 73.2 us -> none  [on_device(): lax.all_gather(cotangent, 'tensor', axis=0, tiled=True)]
    pallas_call x0 -> x8, Pallas kernels: none -> 56.5 us  [the longest x4 31.9 us: add_step(): pl.pallas_call(add_kernel, grid_spec=pltpu.PrefetchScalarGridSpec(num_sca...]
    ppermute x0 -> x12, starting transfers between devices: none -> 21.6 us  [the longest x6 13.9 us: on_device(): lax.ppermute(x, 'tensor', [(i, i + 1) for i in range(step - 1, ranks - 1)])]
    dot_general x2 -> x18, matrix products: 9.78 us -> 24.9 us  [the longest x16 23 us: dot(): lax.dot_general(a, b, (((1,), (0,)), ((), ())), preferred_element_type=jn...]
    mul x4 -> x0, local copies, waits for them, and re-layouts: 13.5 us -> none  [on_device(): blocks * (1.0 - sent_mask[:, None])]
    ppermute x0 -> x12, waiting for transfers between devices: none -> 10.5 us  [the longest x6 10.5 us: on_device(): lax.ppermute(x, 'tensor', [(i, i - 1) for i in range(1, ranks - step + 1)])]
    reshape x1, local copies, waits for them, and re-layouts: 8.91 us -> 0.01 us  [on_device(): return (out[None], summed.reshape(1, regions, caps, LANES))]
    all_to_all x2 -> x0, starting transfers between devices: 8.81 us -> none  [the longest x1 5.2 us: on_device(): lax.all_to_all(offsets.astype(jnp.float32), 'dp', split_axis=0, concat_ax...]
  transfers between devices with their start and end apart: 3 -> 12, of which waited for: 1 -> 3; matrix products, arithmetic and copies ran while one was open for 20% -> 22% of each run, Pallas kernels for 0% -> 33%
where the time goes in v1:
time: 136 us; the launch traced here: 134 us
  Pallas kernels  56.5 us (42%)
  matrix products  24.9 us (18%)
  starting transfers between devices  21.6 us (16%)
  waiting for transfers between devices  10.5 us (8%)
  blocking collectives  9.55 us (7%)
  local copies, waits for them, and re-layouts  8.31 us (6%)
  other arithmetic  1.91 us (1%)
    pallas_call x4, Pallas kernels, add_step(): pl.pallas_call(add_kernel, grid_spec=pltpu.PrefetchScalarGridSpec(num_sca...  31.9 us
    dot_general x16, matrix products, dot(): lax.dot_general(a, b, (((1,), (0,)), ((), ())), preferred_element_type=jn...  23 us
    ppermute x6, starting transfers between devices, on_device(): lax.ppermute(x, 'tensor', [(i, i + 1) for i in range(step - 1, ranks - 1)])  13.9 us
    pallas_call x2, Pallas kernels, last_step(): pl.pallas_call(functools.partial(last_kernel, first=column // LANES), gri...  12.6 us
    pallas_call x2, Pallas kernels, first_step(): pl.pallas_call(first_kernel, grid_spec=pltpu.PrefetchScalarGridSpec(num_s...  12 us
    ppermute x6, waiting for transfers between devices, on_device(): lax.ppermute(x, 'tensor', [(i, i - 1) for i in range(1, ranks - step + 1)])  10.5 us
    all_gather x1, blocking collectives, on_device(): every = lax.all_gather(mine, 'dp', axis=0)  9.55 us
    ppermute x6, starting transfers between devices, on_device(): lax.ppermute(x, 'tensor', [(i, i - 1) for i in range(1, ranks - step + 1)])  7.73 us
  transfers between devices with their start and end apart: 12, of which 3 were waited for; matrix products, arithmetic and copies ran while one was open for 22% of the time, Pallas kernels for 33%

profile of v1, /device:TPU:0, one launch (start us, length us, event | category | flops | bytes accessed | tf_op | source)
XLA Modules:
  0.0 134.4 jit_solution(4289302481525776840)
XLA Ops:
  0.7 2.5 %fusion.68 = (bf16[256,1280]{1,0:T(8,128)(2,1)}, bf16[256,1280]{1,0:T(8,128)(2,1)}) fusion(bf16[256,2560]{1,0:T(8,128)(2,1)} %param.9), kind=kLoop, calls=%fused_computation.88 | loop fusion | bytes 2621440 | tf_op jit(solution)/shard_map/slice | solution.py:149
  3.2 1.3 collective-permute-start.9
  4.4 5.6 %collective-permute-start.6 = (bf16[256,1280]{1,0:T(8,128)(2,1)}, bf16[256,1280]{1,0:T(8,128)(2,1)S(1)}, u32[]{:S(2)}, u32[]{:S(2)}) collective-permute-start(bf16[256,1280]{1,0:T(8,128)(2,1)} %get-tuple-element.12.piece_ref), channel_id=1, source_target_pairs={{0,1},{1,2},{2,3},{4,5},{5,6},{6,7},{8,9},{9,10},{10,11},{12,13},{... | collective-permute-start | bytes 1966088 | tf_op jit(solution)/shard_map/ppermute | solution.py:153
  10.1 1.3 collective-permute-start.3
  11.4 4.6 %collective-permute-start = (bf16[256,1280]{1,0:T(8,128)(2,1)}, bf16[256,1280]{1,0:T(8,128)(2,1)S(1)}, u32[]{:S(2)}, u32[]{:S(2)}) collective-permute-start(bf16[256,1280]{1,0:T(8,128)(2,1)} %get-tuple-element.13.piece_ref), channel_id=1, source_target_pairs={{0,1},{1,2},{2,3},{4,5},{5,6},{6,7},{8,9},{9,10},{10,11},{12,13},{... | collective-permute-start | bytes 1966088 | tf_op jit(solution)/shard_map/ppermute | solution.py:153
  16.0 0.1 add.213
  16.1 0.1 add.214
  16.2 0.1 squeeze.11
  16.3 0.1 iota_compare_fusion.6
  16.3 0.1 copy.35
  16.4 0.4 and_reduce_fusion
  16.8 0.1 copy.36
  16.9 0.1 and.84
  17.0 0.0 copy-start
  17.0 2.9 %fusion.8 = f32[96,1280]{1,0:T(8,128)} fusion(bf16[768,2560]{1,0:T(8,128)(2,1)} %bitcast.43, s32[96]{0:T(128)S(1)} %get-tuple-element.19, pred[96]{0:T(512)(128)(4,1)S(1)} %and.84), kind=kOutput, calls=%fused_computation.16 | convolution fusion | flops 188891136 | bytes 2458080 | tf_op jit(solution)/shard_map/dot_general | solution.py:14
  19.9 2.8 %fusion.6 = f32[96,1280]{1,0:T(8,128)} fusion(bf16[768,2560]{1,0:T(8,128)(2,1)} %bitcast.44, s32[96]{0:T(128)S(1)} %get-tuple-element.19, pred[96]{0:T(512)(128)(4,1)S(1)} %and.84), kind=kOutput, calls=%fused_computation.14 | convolution fusion | flops 188891136 | bytes 2458080 | tf_op jit(solution)/shard_map/dot_general | solution.py:14
  22.8 0.6 convolution_convert_fusion
  23.4 1.7 %copy.34 = bf16[1024,768]{0,1:T(8,128)(2,1)} copy(bf16[1024,768]{1,0:T(8,128)(2,1)S(1)} %copy-done) | data formatting | bytes 3145728 | tf_op args[0]
  25.1 0.1 squeeze.10
  25.2 0.7 pad_add_fusion.index_ref
  25.9 0.1 add.209
  25.9 0.1 add.210
  26.0 6.1 %shard_map.98.acc_ref = f32[768,1280]{1,0:T(8,128)} custom-call(s32[1]{0:T(128)} %bitcast.5.index_ref, bf16[768,1024]{1,0:T(8,128)(2,1)} %bitcast.31, bf16[256,1280]{1,0:T(8,128)(2,1)} %get-tuple-element.12.piece_ref, bf16[768,2560]{1,0:T(8,128)(2,1)} %bitcast.45), custom_call_target="tpu_custom_call" | custom-call | flops 503316480 | bytes 5898240 | tf_op jit(solution)/shard_map/pallas_call | solution.py:52
  32.2 1.0 convolution_add_fusion.7
  33.2 0.1 lt.90
  33.3 1.4 %fusion.13.sent_ref = bf16[768,128]{1,0:T(8,128)(2,1)} fusion(s32[384]{0:T(512)S(1)} %get-tuple-element.17, pred[384]{0:T(512)(128)(4,1)S(1)} %lt.90, s32[384]{0:T(512)S(1)} %get-tuple-element.16), kind=kOutput, calls=%fused_computation.21 | convolution fusion | flops 76234752 | bytes 200064 | tf_op jit(solution)/shard_map/dot_general | solution.py:170
  34.6 5.9 %shard_map.95.acc_ref = f32[768,1280]{1,0:T(8,128)} custom-call(s32[1]{0:T(128)} %bitcast.5.index_ref, bf16[768,1024]{1,0:T(8,128)(2,1)} %bitcast.32, bf16[256,1280]{1,0:T(8,128)(2,1)} %get-tuple-element.13.piece_ref, bf16[768,2560]{1,0:T(8,128)(2,1)} %bitcast.46), custom_call_target="tpu_custom_call" | custom-call | flops 503316480 | bytes 5898240 | tf_op jit(solution)/shard_map/pallas_call | solution.py:52
  40.6 0.6 pad_add_fusion.1.index_ref
  41.2 1.3 convolution_add_fusion.3
  42.5 1.3 collective-permute-start.10
  43.8 0.7 collective-permute-start.7
  44.5 1.3 collective-permute-start.4
  45.8 1.3 fusion.43
  47.2 0.7 collective-permute-start.1
  47.9 1.0 fusion.5
  48.9 2.1 %fusion.41 = f32[96,1280]{1,0:T(8,128)} fusion(bf16[256,1280]{1,0:T(8,128)(2,1)} %collective-permute-done.3.down_ref, bf16[96,1024]{1,0:T(8,128)(2,1)S(1)} %convolution_convert_fusion, s32[]{:T(128)S(6)} %select_n.77), kind=kOutput, calls=%fused_computation.50 | convolution fusion | flops 62914560 | bytes 1196036 | tf_op jit(solution)/shard_map/dot_general | solution.py:14
  51.0 8.0 %shard_map.99.acc_ref = f32[768,1280]{1,0:T(8,128)} custom-call(s32[2]{0:T(128)} %pad_add_fusion.1.index_ref, bf16[768,1024]{1,0:T(8,128)(2,1)} %bitcast.33, bf16[768,1024]{1,0:T(8,128)(2,1)} %bitcast.34, bf16[256,1280]{1,0:T(8,128)(2,1)} %copy-done.3, bf16[256,1280]{1,0:T(8,128)(2,1)} %collective-permute-done.9.down_ref, ...), custom_call_target="tpu_custom_call", output_to_operand_aliasing={{}: (5, {})} | custom-call | flops 1006632960 | bytes 7864320 | tf_op jit(solution)/shard_map/pallas_call | solution.py:75
  59.1 8.0 %shard_map.96.acc_ref = f32[768,1280]{1,0:T(8,128)} custom-call(s32[2]{0:T(128)} %pad_add_fusion.1.index_ref, bf16[768,1024]{1,0:T(8,128)(2,1)} %bitcast.35, bf16[768,1024]{1,0:T(8,128)(2,1)} %bitcast.36, bf16[256,1280]{1,0:T(8,128)(2,1)} %copy-done.2, bf16[256,1280]{1,0:T(8,128)(2,1)} %collective-permute-done.3.down_ref, ...), custom_call_target="tpu_custom_call", output_to_operand_aliasing={{}: (5, {})} | custom-call | flops 1006632960 | bytes 7864320 | tf_op jit(solution)/shard_map/pallas_call | solution.py:75
  67.0 1.5 %fusion.2 = f32[96,1280]{1,0:T(8,128)S(1)} fusion(f32[96,1280]{1,0:T(8,128)} %fusion.41, f32[96,1280]{1,0:T(8,128)S(1)} %convolution_add_fusion.3, bf16[256,1280]{1,0:T(8,128)(2,1)} %copy-done.2, bf16[96,1024]{1,0:T(8,128)(2,1)S(1)} %convolution_convert_fusion, s32[]{:T(128)S(6)} %select_n.76), kind=kOutput, calls=%fused_computation.5 | convolution fusion | flops 63160320 | bytes 2179076 | tf_op jit(solution)/shard_map/dot_general | solution.py:14
  68.6 1.3 collective-permute-start.11
  69.9 1.5 %collective-permute-start.8 = (bf16[256,1280]{1,0:T(8,128)(2,1)S(1)}, bf16[256,1280]{1,0:T(8,128)(2,1)}, u32[]{:S(2)}, u32[]{:S(2)}) collective-permute-start(bf16[256,1280]{1,0:T(8,128)(2,1)S(1)} %collective-permute-done.7.up_ref), channel_id=1, source_target_pairs={{2,3},{6,7},{10,11},{14,15},{18,19},{22,23},{26,27},{30,31}} | collective-permute-start | bytes 1966088 | tf_op jit(solution)/shard_map/ppermute | solution.py:153
  71.4 3.5 %collective-permute-done.4.down_ref = bf16[256,1280]{1,0:T(8,128)(2,1)} collective-permute-done((bf16[256,1280]{1,0:T(8,128)(2,1)}, bf16[256,1280]{1,0:T(8,128)(2,1)}, u32[]{:S(2)}, u32[]{:S(2)}) %collective-permute-start.4) | collective-permute-done | bytes 655392 | tf_op jit(solution)/shard_map/ppermute | solution.py:156
  75.0 1.3 collective-permute-start.5
  76.2 1.3 fusion.37
  77.6 0.7 collective-permute-start.2
  78.3 1.1 fusion.4
  79.4 1.3 fusion.35
  80.7 0.3 fusion.1
  81.0 8.0 %shard_map.100.acc_ref = f32[768,1280]{1,0:T(8,128)} custom-call(s32[2]{0:T(128)} %pad_add_fusion.index_ref, bf16[768,1024]{1,0:T(8,128)(2,1)} %bitcast.37, bf16[768,1024]{1,0:T(8,128)(2,1)} %bitcast.38, bf16[256,1280]{1,0:T(8,128)(2,1)} %copy-done.4, bf16[256,1280]{1,0:T(8,128)(2,1)} %collective-permute-done.10.down_ref, ...), custom_call_target="tpu_custom_call", output_to_operand_aliasing={{}: (5, {})} | custom-call | flops 1006632960 | bytes 7864320 | tf_op jit(solution)/shard_map/pallas_call | solution.py:75
  89.0 8.0 %shard_map.97.acc_ref = f32[768,1280]{1,0:T(8,128)} custom-call(s32[2]{0:T(128)} %pad_add_fusion.index_ref, bf16[768,1024]{1,0:T(8,128)(2,1)} %bitcast.39, bf16[768,1024]{1,0:T(8,128)(2,1)} %bitcast.40, bf16[256,1280]{1,0:T(8,128)(2,1)} %copy-done.5, bf16[256,1280]{1,0:T(8,128)(2,1)} %collective-permute-done.4.down_ref, ...), custom_call_target="tpu_custom_call", output_to_operand_aliasing={{}: (5, {})} | custom-call | flops 1006632960 | bytes 7864320 | tf_op jit(solution)/shard_map/pallas_call | solution.py:75
  97.0 0.7 collective-permute-done.11.down_ref
  97.7 1.3 fusion.31
  99.0 2.3 %fusion.3 = f32[96,1280]{1,0:T(8,128)} fusion(f32[96,1280]{1,0:T(8,128)S(1)} %fusion.31, f32[96,1280]{1,0:T(8,128)} %fusion.4, bf16[256,1280]{1,0:T(8,128)(2,1)} %collective-permute-done.8.up_ref, bf16[96,1024]{1,0:T(8,128)(2,1)S(1)} %convolution_convert_fusion, s32[]{:T(128)S(6)} %select_n.80), kind=kOutput, calls=%fused_computation.8 | convolution fusion | flops 63160320 | bytes 2179076 | tf_op jit(solution)/shard_map/dot_general | solution.py:14
  101.3 1.3 copy.37
  102.6 6.3 %collective-permute-done.5.down_ref = bf16[256,1280]{1,0:T(8,128)(2,1)S(1)} collective-permute-done((bf16[256,1280]{1,0:T(8,128)(2,1)}, bf16[256,1280]{1,0:T(8,128)(2,1)S(1)}, u32[]{:S(2)}, u32[]{:S(2)}) %collective-permute-start.5) | collective-permute-done | bytes 655392 | tf_op jit(solution)/shard_map/ppermute | solution.py:156
  108.8 0.2 fusion.29
  109.1 1.0 fusion
  110.1 1.3 copy.38
  111.4 0.1 multiply_reduce_fusion
  111.6 0.1 copy.39
  111.7 9.5 %all-gather = f32[768,128]{1,0:T(8,128)S(1)} all-gather(f32[96,128]{1,0:T(8,128)S(1)} %copy.39), channel_id=2, replica_groups=mesh['dp'=8,'tensor'=4] {'dp'}, dimensions={0}, use_global_device_ids=true | all-gather | bytes 442368 | tf_op jit(solution)/shard_map/all_gather | solution.py:213
  121.2 0.6 copy.40
  121.9 6.3 %shard_map.101.rest_0_ = bf16[768,2560]{1,0:T(8,128)(2,1)} custom-call(s32[1]{0:T(128)} %bitcast.index_ref, bf16[768,1024]{1,0:T(8,128)(2,1)} %bitcast.41, bf16[256,1280]{1,0:T(8,128)(2,1)} %collective-permute-done.8.up_ref, bf16[256,1280]{1,0:T(8,128)(2,1)} %collective-permute-done.11.down_ref, f32[768,1280]{1,0:T(8,128)} %shard_map.100.acc_ref, ...), custom_call_target="tpu_custom_call" | custom-call | flops 503316480 | bytes 5898240 | tf_op jit(solution)/shard_map/pallas_call | solution.py:115
  128.2 6.3 %shard_map.102 = bf16[768,2560]{1,0:T(8,128)(2,1)} custom-call(s32[1]{0:T(128)} %bitcast.index_ref, bf16[768,1024]{1,0:T(8,128)(2,1)} %bitcast.42, bf16[256,1280]{1,0:T(8,128)(2,1)} %copy-done.6, bf16[256,1280]{1,0:T(8,128)(2,1)} %copy-done.7, f32[768,1280]{1,0:T(8,128)} %shard_map.97.acc_ref, ...), custom_call_target="tpu_custom_call", output_to_operand_aliasing={{}: (6, {})} | custom-call | flops 503316480 | bytes 5898240 | tf_op jit(solution)/shard_map/pallas_call | solution.py:115
  (48 shorter events, 0.2 us)
Async XLA Ops:
  0.6 15.4 %copy-start.13 = (s32[9]{0:T(128)S(1)}, s32[9]{0:T(128)}, u32[]{:S(2)}) copy-start(s32[9]{0:T(128)} %param.15) | copy-start | bytes 112
  0.6 15.5 %copy-start.11 = (s32[1,8,12]{2,1,0:T(8,128)S(1)}, s32[1,8,12]{2,1,0:T(8,128)}, u32[]{:S(2)}) copy-start(s32[1,8,12]{2,1,0:T(8,128)} %param.13) | copy-start | bytes 1156
  0.7 15.6 %copy-start.15 = (s32[1,1,8]{2,1,0:T(1,128)S(1)}, s32[1,1,8]{2,1,0:T(1,128)}, u32[]{:S(2)}) copy-start(s32[1,1,8]{2,1,0:T(1,128)} %param.12) | copy-start | bytes 100
  0.7 15.8 %copy-start.12 = (s32[1,1,8,48]{3,2,1,0:T(8,128)S(1)}, s32[1,1,8,48]{3,2,1,0:T(8,128)}, u32[]{:S(2)}) copy-start(s32[1,1,8,48]{3,2,1,0:T(8,128)} %param.11) | copy-start | bytes 4612
  0.7 16.1 %copy-start.14 = (s32[1,8]{1,0:T(1,128)S(1)}, s32[1,8]{1,0:T(1,128)}, u32[]{:S(2)}) copy-start(s32[1,8]{1,0:T(1,128)} %param.14) | copy-start | bytes 100
  3.2 39.3 %collective-permute-start.9 = (bf16[256,1280]{1,0:T(8,128)(2,1)}, bf16[256,1280]{1,0:T(8,128)(2,1)}, u32[]{:S(2)}, u32[]{:S(2)}) collective-permute-start(bf16[256,1280]{1,0:T(8,128)(2,1)} %get-tuple-element.12.piece_ref), channel_id=1, source_target_pairs={{1,0},{2,1},{3,2},{5,4},{6,5},{7,6},{9,8},{10,9},{11,10},{13,12},{... | collective-permute-start | bytes 1966088 | tf_op jit(solution)/shard_map/ppermute | solution.py:156
  4.4 39.3 %collective-permute-start.6 = (bf16[256,1280]{1,0:T(8,128)(2,1)}, bf16[256,1280]{1,0:T(8,128)(2,1)S(1)}, u32[]{:S(2)}, u32[]{:S(2)}) collective-permute-start(bf16[256,1280]{1,0:T(8,128)(2,1)} %get-tuple-element.12.piece_ref), channel_id=1, source_target_pairs={{0,1},{1,2},{2,3},{4,5},{5,6},{6,7},{8,9},{9,10},{10,11},{12,13},{... | collective-permute-start | bytes 1966088 | tf_op jit(solution)/shard_map/ppermute | solution.py:153
  10.1 34.4 %collective-permute-start.3 = (bf16[256,1280]{1,0:T(8,128)(2,1)}, bf16[256,1280]{1,0:T(8,128)(2,1)}, u32[]{:S(2)}, u32[]{:S(2)}) collective-permute-start(bf16[256,1280]{1,0:T(8,128)(2,1)} %get-tuple-element.13.piece_ref), channel_id=1, source_target_pairs={{1,0},{2,1},{3,2},{5,4},{6,5},{7,6},{9,8},{10,9},{11,10},{13,12},{... | collective-permute-start | bytes 1966088 | tf_op jit(solution)/shard_map/ppermute | solution.py:156
  11.4 35.8 %collective-permute-start = (bf16[256,1280]{1,0:T(8,128)(2,1)}, bf16[256,1280]{1,0:T(8,128)(2,1)S(1)}, u32[]{:S(2)}, u32[]{:S(2)}) collective-permute-start(bf16[256,1280]{1,0:T(8,128)(2,1)} %get-tuple-element.13.piece_ref), channel_id=1, source_target_pairs={{0,1},{1,2},{2,3},{4,5},{5,6},{6,7},{8,9},{9,10},{10,11},{12,13},{... | collective-permute-start | bytes 1966088 | tf_op jit(solution)/shard_map/ppermute | solution.py:153
  17.0 5.8 %copy-start = (bf16[1024,768]{1,0:T(8,128)(2,1)S(1)}, bf16[1024,768]{1,0:T(8,128)(2,1)}, u32[]{:S(2)}) copy-start(bf16[1024,768]{1,0:T(8,128)(2,1)} %param.8) | copy-start | bytes 4718596
  26.0 6.1 %copy-start.1 = (bf16[256,2560]{1,0:T(8,128)(2,1)S(1)}, bf16[256,2560]{1,0:T(8,128)(2,1)}, u32[]{:S(2)}) copy-start(bf16[256,2560]{1,0:T(8,128)(2,1)} %param.9) | copy-start | bytes 3932164
  26.0 6.1 %copy-start.10 = (f32[96,1280]{1,0:T(8,128)S(1)}, f32[96,1280]{1,0:T(8,128)}, u32[]{:S(2)}) copy-start(f32[96,1280]{1,0:T(8,128)} %fusion.8) | copy-start | bytes 1474564
  40.6 7.3 %copy-start.8 = (f32[96,1280]{1,0:T(8,128)S(1)}, f32[96,1280]{1,0:T(8,128)}, u32[]{:S(2)}) copy-start(f32[96,1280]{1,0:T(8,128)} %convolution_add_fusion.7) | copy-start | bytes 1474564
  42.5 26.1 %collective-permute-start.10 = (bf16[256,1280]{1,0:T(8,128)(2,1)}, bf16[256,1280]{1,0:T(8,128)(2,1)}, u32[]{:S(2)}, u32[]{:S(2)}) collective-permute-start(bf16[256,1280]{1,0:T(8,128)(2,1)} %collective-permute-done.9.down_ref), channel_id=1, source_target_pairs={{1,0},{2,1},{5,4},{6,5},{9,8},{10,9},{13,12},{14,13},{17,16},{18,1... | collective-permute-start | bytes 1966088 | tf_op jit(solution)/shard_map/ppermute | solution.py:156
  43.8 7.3 %copy-start.3 = (bf16[256,1280]{1,0:T(8,128)(2,1)}, bf16[256,1280]{1,0:T(8,128)(2,1)S(1)}, u32[]{:S(2)}) copy-start(bf16[256,1280]{1,0:T(8,128)(2,1)S(1)} %collective-permute-done.6.up_ref) | copy-start | bytes 1966084
  43.8 26.1 %collective-permute-start.7 = (bf16[256,1280]{1,0:T(8,128)(2,1)S(1)}, bf16[256,1280]{1,0:T(8,128)(2,1)S(1)}, u32[]{:S(2)}, u32[]{:S(2)}) collective-permute-start(bf16[256,1280]{1,0:T(8,128)(2,1)S(1)} %collective-permute-done.6.up_ref), channel_id=1, source_target_pairs={{1,2},{2,3},{5,6},{6,7},{9,10},{10,11},{13,14},{14,15},{17,18},{18... | collective-permute-start | bytes 1966088 | tf_op jit(solution)/shard_map/ppermute | solution.py:153
  44.5 30.5 %collective-permute-start.4 = (bf16[256,1280]{1,0:T(8,128)(2,1)}, bf16[256,1280]{1,0:T(8,128)(2,1)}, u32[]{:S(2)}, u32[]{:S(2)}) collective-permute-start(bf16[256,1280]{1,0:T(8,128)(2,1)} %collective-permute-done.3.down_ref), channel_id=1, source_target_pairs={{1,0},{2,1},{5,4},{6,5},{9,8},{10,9},{13,12},{14,13},{17,16},{18,1... | collective-permute-start | bytes 1966088 | tf_op jit(solution)/shard_map/ppermute | solution.py:156
  47.2 11.9 %copy-start.2 = (bf16[256,1280]{1,0:T(8,128)(2,1)}, bf16[256,1280]{1,0:T(8,128)(2,1)S(1)}, u32[]{:S(2)}) copy-start(bf16[256,1280]{1,0:T(8,128)(2,1)S(1)} %collective-permute-done.up_ref) | copy-start | bytes 1966084
  47.2 30.4 %collective-permute-start.1 = (bf16[256,1280]{1,0:T(8,128)(2,1)S(1)}, bf16[256,1280]{1,0:T(8,128)(2,1)S(1)}, u32[]{:S(2)}, u32[]{:S(2)}) collective-permute-start(bf16[256,1280]{1,0:T(8,128)(2,1)S(1)} %collective-permute-done.up_ref), channel_id=1, source_target_pairs={{1,2},{2,3},{5,6},{6,7},{9,10},{10,11},{13,14},{14,15},{17,18},{18... | collective-permute-start | bytes 1966088 | tf_op jit(solution)/shard_map/ppermute | solution.py:153
  67.0 11.3 %copy-start.9 = (f32[96,1280]{1,0:T(8,128)S(1)}, f32[96,1280]{1,0:T(8,128)}, u32[]{:S(2)}) copy-start(f32[96,1280]{1,0:T(8,128)} %fusion.5) | copy-start | bytes 1474564
  68.6 29.1 %collective-permute-start.11 = (bf16[256,1280]{1,0:T(8,128)(2,1)}, bf16[256,1280]{1,0:T(8,128)(2,1)}, u32[]{:S(2)}, u32[]{:S(2)}) collective-permute-start(bf16[256,1280]{1,0:T(8,128)(2,1)} %collective-permute-done.10.down_ref), channel_id=1, source_target_pairs={{1,0},{5,4},{9,8},{13,12},{17,16},{21,20},{25,24},{29,28}} | collective-permute-start | bytes 1966088 | tf_op jit(solution)/shard_map/ppermute | solution.py:156
  69.9 10.9 %copy-start.4 = (bf16[256,1280]{1,0:T(8,128)(2,1)}, bf16[256,1280]{1,0:T(8,128)(2,1)S(1)}, u32[]{:S(2)}) copy-start(bf16[256,1280]{1,0:T(8,128)(2,1)S(1)} %collective-permute-done.7.up_ref) | copy-start | bytes 1966084
  69.9 29.1 %collective-permute-start.8 = (bf16[256,1280]{1,0:T(8,128)(2,1)S(1)}, bf16[256,1280]{1,0:T(8,128)(2,1)}, u32[]{:S(2)}, u32[]{:S(2)}) collective-permute-start(bf16[256,1280]{1,0:T(8,128)(2,1)S(1)} %collective-permute-done.7.up_ref), channel_id=1, source_target_pairs={{2,3},{6,7},{10,11},{14,15},{18,19},{22,23},{26,27},{30,31}} | collective-permute-start | bytes 1966088 | tf_op jit(solution)/shard_map/ppermute | solution.py:153
  75.0 33.9 %collective-permute-start.5 = (bf16[256,1280]{1,0:T(8,128)(2,1)}, bf16[256,1280]{1,0:T(8,128)(2,1)S(1)}, u32[]{:S(2)}, u32[]{:S(2)}) collective-permute-start(bf16[256,1280]{1,0:T(8,128)(2,1)} %collective-permute-done.4.down_ref), channel_id=1, source_target_pairs={{1,0},{5,4},{9,8},{13,12},{17,16},{21,20},{25,24},{29,28}} | collective-permute-start | bytes 1966088 | tf_op jit(solution)/shard_map/ppermute | solution.py:156
  77.6 3.4 %copy-start.5 = (bf16[256,1280]{1,0:T(8,128)(2,1)}, bf16[256,1280]{1,0:T(8,128)(2,1)S(1)}, u32[]{:S(2)}) copy-start(bf16[256,1280]{1,0:T(8,128)(2,1)S(1)} %collective-permute-done.1.up_ref) | copy-start | bytes 1966084
  77.6 31.4 %collective-permute-start.2 = (bf16[256,1280]{1,0:T(8,128)(2,1)S(1)}, bf16[256,1280]{1,0:T(8,128)(2,1)S(1)}, u32[]{:S(2)}, u32[]{:S(2)}) collective-permute-start(bf16[256,1280]{1,0:T(8,128)(2,1)S(1)} %collective-permute-done.1.up_ref), channel_id=1, source_target_pairs={{2,3},{6,7},{10,11},{14,15},{18,19},{22,23},{26,27},{30,31}} | collective-permute-start | bytes 1966088 | tf_op jit(solution)/shard_map/ppermute | solution.py:153
  108.8 2.6 %copy-start.7 = (bf16[256,1280]{1,0:T(8,128)(2,1)}, bf16[256,1280]{1,0:T(8,128)(2,1)S(1)}, u32[]{:S(2)}) copy-start(bf16[256,1280]{1,0:T(8,128)(2,1)S(1)} %collective-permute-done.5.down_ref) | copy-start | bytes 1966084
  109.1 2.5 %copy-start.6 = (bf16[256,1280]{1,0:T(8,128)(2,1)}, bf16[256,1280]{1,0:T(8,128)(2,1)S(1)}, u32[]{:S(2)}) copy-start(bf16[256,1280]{1,0:T(8,128)(2,1)S(1)} %collective-permute-done.2.up_ref) | copy-start | bytes 1966084
